TPU v7x, 32 devices: a whole 2x2x4 slice. The times are simulated.
32 devices in a mesh: ctx: 16 (over z, y, core), head: 2 (over x).
Axes of the slice: x: 2, y: 2, z: 4, core: 2. Of those that a mesh axis runs over, the one named last changes fastest.
Arguments:
- patch_hidden: bfloat16 [1024, 4096], P('ctx', 'head'), may hold values from -6 to 6
- queries: bfloat16 [1024, 32, 128], P('ctx', 'head'), may hold values from -6 to 6
- new_keys: bfloat16 [1024, 32, 128], P('ctx', 'head'), may hold values from -6 to 6
- new_values: bfloat16 [1024, 32, 128], P('ctx', 'head'), may hold values from -6 to 6
- cache_keys: bfloat16 [16384, 32, 128], P('ctx', 'head'), may hold values from -6 to 6
- cache_values: bfloat16 [16384, 32, 128], P('ctx', 'head'), may hold values from -6 to 6
- cache_request: int32 [16384], P('ctx'), may hold values from 0 to 7, never falling along the last dimension, each value on 1 to 4096 neighbouring positions
- new_request: int32 [1024], replicated, may hold values from 0 to 7, as said below
- out_weight: bfloat16 [32, 128, 4096], P('head'), may hold values from -0.375 to 0.375
- norm_gain: float32 [4096], replicated, may hold values from 0.1 to 1.9
- dec_kv_weight: bfloat16 [4096, 2, 1024], P(None, None, 'head'), may hold values from -0.09375 to 0.09375
- dec_query_weight: bfloat16 [1024, 1024], P(None, 'head'), may hold values from -0.1875 to 0.1875
- query_gain: float32 [64], replicated, may hold values from 0.1 to 1.9
- key_gain: float32 [64], replicated, may hold values from 0.1 to 1.9
- dec_out_weight: bfloat16 [1024, 1024], P('head'), may hold values from -0.75 to 0.75
- byte_states: bfloat16 [4096, 1024], P('ctx'), may hold values from -6 to 6
- byte_patch: int32 [4096], P('ctx'), may hold values from 0 to 1023, never falling along the last dimension, each value on 1 to 8 neighbouring positions
Outputs:
- patch_out: bfloat16 [1024, 4096], P('ctx', 'head')
- byte_out: bfloat16 [4096, 1024], P('ctx', 'head')
Inputs may be any that keep to these rules, and one draw needn't show every extreme that they name: `new_request`: never falls along the patches; every request of 0 to 7 has an even number, two or more, of new patches. `cache_request`: never falls along the cached patches; every request has one or more cached patches. `byte_patch`: never falls along the bytes; every new patch owns one or more bytes.
All inputs are finite; a program needn't handle non-finite values.
Results may differ from a plain program's by a relative error of at most 0.017.
Values may be sent and summed in bfloat16 or wider, within the bound.
No kernel may reach another device: no remote copies, remote signals or barrier semaphores. Data moves between devices by JAX's collectives and lax.ppermute only.
A program may use at most 128 MiB of HBM per device.

v0:
```python
import jax
import jax.numpy as jnp
from jax import lax
from jax.sharding import PartitionSpec as P

DEC_DH = 64


def row_norm(values, gain_values, epsilon):
    meansq = jnp.mean(values * values, axis=-1, keepdims=True)
    return values * lax.rsqrt(meansq + epsilon) * gain_values


def per_device(
    patch_hidden,
    queries,
    new_keys,
    new_values,
    cache_keys,
    cache_values,
    cache_request,
    new_request,
    out_weight,
    norm_gain,
    dec_kv_weight,
    dec_query_weight,
    query_gain,
    key_gain,
    dec_out_weight,
    byte_states,
    byte_patch,
):
    new_rows, local_heads, head_size = queries.shape
    cache_rows = cache_keys.shape[0]
    total_rows = new_request.shape[0]
    ctx_index = lax.axis_index("ctx")
    head_index = lax.axis_index("head")
    first_new = ctx_index * new_rows
    all_keys = jnp.transpose(jnp.concatenate([cache_keys, new_keys], 0), (1, 0, 2))
    all_values = jnp.transpose(jnp.concatenate([cache_values, new_values], 0), (1, 0, 2))
    own_request = lax.dynamic_slice_in_dim(new_request, first_new, new_rows)
    local_request = jnp.concatenate([cache_request, own_request])
    local_position = jnp.concatenate(
        [jnp.full((cache_rows,), -1, jnp.int32), first_new + jnp.arange(new_rows, dtype=jnp.int32)]
    )
    score_scale = head_size ** (-0.5)
    portion = lax.all_gather(queries, "ctx", axis=0, tiled=True)
    row_count = portion.shape[0]
    piece_index = jnp.arange(row_count, dtype=jnp.int32)
    visible = (local_request[None, :] == new_request[:, None]) & (
        local_position[None, :] <= piece_index[:, None]
    )

    def one_head(inputs):
        query_head, key_head, value_head = inputs
        scores = (
            jnp.einsum("qd,kd->qk", query_head, key_head, preferred_element_type=jnp.float32)
            * score_scale
        )
        highest = jnp.max(jnp.where(visible, scores, -1e30), axis=1)
        weights = jnp.where(visible, jnp.exp(scores - highest[:, None]), 0.0)
        mixed_rows = jnp.dot(
            weights.astype(jnp.bfloat16), value_head, preferred_element_type=jnp.float32
        )
        return (mixed_rows, jnp.sum(weights, axis=1), highest)

    pieces = lax.map(one_head, (jnp.transpose(portion, (1, 0, 2)), all_keys, all_values))
    partial_out, partial_total, partial_max = tuple((part_values for part_values in pieces))
    highest = lax.pmax(partial_max, "ctx")
    factor = jnp.exp(partial_max - highest)
    summed_out, summed_total = (
        lax.psum_scatter(partial_out * factor[..., None], "ctx", scatter_dimension=1, tiled=True),
        lax.psum_scatter(partial_total * factor, "ctx", scatter_dimension=1, tiled=True),
    )
    attended = (summed_out / summed_total[..., None]).astype(jnp.bfloat16)
    flattened = jnp.transpose(attended, (1, 0, 2)).reshape(new_rows, local_heads * head_size)
    head_terms = jnp.dot(
        flattened,
        out_weight.reshape(local_heads * head_size, -1),
        preferred_element_type=jnp.float32,
    )
    model_width = head_terms.shape[1]
    slice_width = patch_hidden.shape[1]
    projected = lax.psum_scatter(head_terms, "head", scatter_dimension=1, tiled=True)
    patch_out = (patch_hidden.astype(jnp.float32) + projected).astype(jnp.bfloat16)
    widened = patch_out.astype(jnp.float32)
    squares = lax.psum(jnp.sum(widened * widened, axis=1), "head")
    gain_part = lax.dynamic_slice_in_dim(norm_gain, head_index * slice_width, slice_width)
    normed_part = (widened * lax.rsqrt(squares / model_width + 1e-05)[:, None] * gain_part).astype(
        jnp.bfloat16
    )
    normed = lax.all_gather(normed_part, "head", axis=1, tiled=True)
    dec_width = dec_kv_weight.shape[2]
    dec_heads = dec_width // DEC_DH
    patch_proj = jnp.dot(
        normed,
        dec_kv_weight.reshape(dec_kv_weight.shape[0], 2 * dec_width),
        preferred_element_type=jnp.float32,
    )
    patch_keys = row_norm(
        patch_proj[:, :dec_width].reshape(new_rows, dec_heads, DEC_DH), key_gain, 1e-06
    ).astype(jnp.bfloat16)
    patch_values = (
        patch_proj[:, dec_width:].astype(jnp.bfloat16).reshape(new_rows, dec_heads, DEC_DH)
    )
    byte_rows = byte_states.shape[0]
    query_proj = jnp.dot(byte_states, dec_query_weight, preferred_element_type=jnp.float32).reshape(
        byte_rows, dec_heads, DEC_DH
    )
    byte_query = row_norm(query_proj, query_gain, 1e-06).astype(jnp.bfloat16)
    table_index = jnp.arange(total_rows, dtype=jnp.int32)
    owner_table = table_index[None, :] == byte_patch[:, None]
    byte_request = jnp.sum(jnp.where(owner_table, new_request[None, :], 0), axis=1)
    dec_scale = DEC_DH ** (-0.5)
    piece_keys = lax.all_gather(patch_keys, "ctx", axis=0, tiled=True)
    piece_values = lax.all_gather(patch_values, "ctx", axis=0, tiled=True)
    row_count = piece_keys.shape[0]
    patch_index = jnp.arange(row_count, dtype=jnp.int32)
    fold_visible = (new_request[None, :] == byte_request[:, None]) & (
        patch_index[None, :] <= byte_patch[:, None]
    )
    scores = (
        jnp.einsum("bhd,jhd->hbj", byte_query, piece_keys, preferred_element_type=jnp.float32)
        * dec_scale
    )
    weights = jnp.where(fold_visible[None], jnp.exp(scores), 0.0)
    mixed_rows = jnp.einsum(
        "hbj,jhd->bhd",
        weights.astype(jnp.bfloat16),
        piece_values,
        preferred_element_type=jnp.float32,
    )
    denominator = jnp.transpose(jnp.sum(weights, axis=2))
    byte_mixed = (
        (mixed_rows / denominator[..., None]).astype(jnp.bfloat16).reshape(byte_rows, dec_width)
    )
    byte_terms = jnp.dot(byte_mixed, dec_out_weight, preferred_element_type=jnp.float32)
    byte_sum = lax.psum_scatter(byte_terms, "head", scatter_dimension=1, tiled=True)
    out_width = byte_sum.shape[1]
    own_states = lax.dynamic_slice_in_dim(byte_states, head_index * out_width, out_width, 1)
    byte_out = (own_states.astype(jnp.float32) + byte_sum).astype(jnp.bfloat16)
    return (patch_out, byte_out)


def solution(mesh):
    placed = (
        P("ctx", "head"),
        P("ctx", "head", None),
        P("ctx", "head", None),
        P("ctx", "head", None),
        P("ctx", "head", None),
        P("ctx", "head", None),
        P("ctx"),
        P(),
        P("head", None, None),
        P(),
        P(None, None, "head"),
        P(None, "head"),
        P(),
        P(),
        P("head", None),
        P("ctx", None),
        P("ctx"),
    )
    return jax.shard_map(
        per_device,
        mesh=mesh,
        in_specs=placed,
        out_specs=(P("ctx", "head"), P("ctx", "head")),
        check_vma=False,
    )
```

profile of v0, /device:TPU:0, one launch (start us, length us, event | category | flops | bytes accessed | tf_op | source)
XLA Modules:
  0.0 629.6 jit_solution(7363839396870362774)
XLA Ops:
  7.2 1.8 copy.44
  9.2 5.4 copy.45
  14.6 3.1 copy.47
  18.0 6.0 maximum_bitcast_fusion
  24.0 39.9 %all-gather.4.cloned.1.call-done = bf16[1024,16,128]{2,0,1:T(8,128)(2,1)} async-done(((bf16[64,16,128]{2,0,1:T(8,128)(2,1)}), bf16[1024,16,128]{2,0,1:T(8,128)(2,1)}) %all-gather.4.cloned.1.call-update) | async-done | bytes 4194320 | tf_op jit(solution)/shard_map/all_gather | solution.py:47
  63.9 143.5 %while.15 = (s32[]{:T(128)}, f32[16,1024,128]{2,1,0:T(8,128)}, f32[16,1024]{1,0:T(8,128)S(1)}, f32[16,1024]{1,0:T(8,128)}, bf16[16,1024,128]{2,1,0:T(8,128)(2,1)...) while((s32[]{:T(128)}, f32[16,1024,128]{2,1,0:T(8,128)}, ...), condition=%wide.region_3.4_spmd.clone, body=%wide.region_0.3_spmd.clone.sunk | while | flops 590477312 | bytes 14786173 | solution.py:67
  63.9 2.5 select_reduce_fusion.3
  66.4 3.4 fusion.74
  69.8 1.5 fusion.75
  72.9 2.5 select_reduce_fusion.3
  75.4 3.4 fusion.74
  78.7 1.5 fusion.75
  81.8 2.5 select_reduce_fusion.3
  84.3 3.4 fusion.74
  87.7 1.5 fusion.75
  90.8 2.5 select_reduce_fusion.3
  93.3 3.4 fusion.74
  96.7 1.5 fusion.75
  99.7 2.5 select_reduce_fusion.3
  102.2 3.4 fusion.74
  105.6 1.5 fusion.75
  108.7 2.5 select_reduce_fusion.3
  111.2 3.4 fusion.74
  114.6 1.5 fusion.75
  117.7 2.5 select_reduce_fusion.3
  120.2 3.4 fusion.74
  123.6 1.5 fusion.75
  126.7 2.5 select_reduce_fusion.3
  129.1 3.4 fusion.74
  132.5 1.5 fusion.75
  135.6 2.5 select_reduce_fusion.3
  138.1 3.4 fusion.74
  144.6 2.5 select_reduce_fusion.3
  147.1 3.4 fusion.74
  150.5 1.5 fusion.75
  153.5 2.5 select_reduce_fusion.3
  156.0 3.4 fusion.74
  159.4 1.5 fusion.75
  162.5 2.5 select_reduce_fusion.3
  165.0 3.4 fusion.74
  171.5 2.5 select_reduce_fusion.3
  174.0 3.4 fusion.74
  180.4 2.5 select_reduce_fusion.3
  182.9 3.4 fusion.74
  189.4 2.5 select_reduce_fusion.3
  191.9 3.4 fusion.74
  198.4 2.5 select_reduce_fusion.3
  200.9 3.4 fusion.74
  207.4 84.9 %all-reduce.3.cloned.1.call-done = f32[16,1024]{1,0:T(8,128)} async-done(((f32[16,1024]{1,0:T(8,128)}), f32[16,1024]{1,0:T(8,128)}) %all-reduce.3.cloned.1.call-update) | async-done | bytes 65552 | tf_op jit(solution)/shard_map/pmax | solution.py:69
  294.3 7.9 %broadcast_multiply_fusion = f32[16,1024,128]{2,1,0:T(8,128)} fusion(f32[16,1024,128]{2,1,0:T(8,128)} %get-tuple-element.46, f32[16,1024]{1,0:T(8,128)S(1)} %get-tuple-element.97), kind=kLoop, calls=%fused_computation.29 | loop fusion | flops 2097152 | bytes 16842752 | tf_op jit(solution)/shard_map/mul | solution.py:72
  302.3 51.3 %reduce-scatter.13.cloned.1.call-done = f32[64,16]{1,0:T(8,128)} async-done(((f32[1024,16]{1,0:T(8,128)}), f32[64,16]{1,0:T(8,128)}) %reduce-scatter.13.cloned.1.call-update) | async-done | bytes 4112
  354.5 105.9 %reduce-scatter.7.cloned.1.call-done = f32[16,64,128]{2,1,0:T(8,128)} async-done(((f32[16,1024,128]{2,1,0:T(8,128)}), f32[16,64,128]{2,1,0:T(8,128)}) %reduce-scatter.7.cloned.1.call-update) | async-done | bytes 524304 | tf_op jit(solution)/shard_map/reduce_scatter | solution.py:72
  460.3 10.1 %convolution_bitcast_fusion = f32[64,4096]{1,0:T(8,128)} fusion(bf16[16,128,4096]{2,1,0:T(8,128)(2,1)} %param.27, f32[16,64,128]{2,1,0:T(8,128)} %reduce-scatter.7.cloned.1.call-done, f32[16,64]{1,0:T(8,128)S(1)} %copy.55), kind=kOutput, calls=%fused_computation.23 | convolution fusion | flops 1074003968 | bytes 18354176 | tf_op jit(solution)/shard_map/dot_general | solution.py:77
  470.7 9.4 %copy.56 = bf16[512,8,2,512]{3,1,2,0:T(8,128)(2,1)} copy(bf16[512,8,2,512]{3,2,1,0:T(2,128)(2,1)} %bitcast.64) | data formatting | bytes 16777216
  480.1 10.5 %reduce-scatter.9.cloned.1.call-done = f32[64,2048]{1,0:T(8,128)} async-done(((f32[64,4096]{1,0:T(8,128)}), f32[64,2048]{1,0:T(8,128)}) %reduce-scatter.9.cloned.1.call-update) | async-done | bytes 524304 | tf_op jit(solution)/shard_map/reduce_scatter | solution.py:84
  491.9 4.9 psum.7
  496.9 7.4 %all_gather.13 = bf16[64,4096]{1,0:T(8,128)(2,1)S(1)} all-gather(bf16[64,2048]{1,0:T(8,128)(2,1)S(1)} %fusion.48), channel_id=1, replica_groups=mesh['ctx'=16,'head'=2] {'head'}, dimensions={1}, use_global_device_ids=true | all-gather | bytes 786432 | tf_op jit(solution)/shard_map/all_gather | solution.py:92
  504.4 5.1 fusion.58
  512.8 39.5 %all-gather.8.cloned.1.call-done = bf16[1024,8,64]{2,0,1:T(8,128)(2,1)} async-done(((bf16[64,8,64]{2,0,1:T(8,128)(2,1)}), bf16[1024,8,64]{2,0,1:T(8,128)(2,1)}) %all-gather.8.cloned.1.call-update) | async-done | bytes 1048592 | tf_op jit(solution)/shard_map/all_gather | solution.py:115
  552.3 7.1 %fusion.22 = (f32[8,256]{1,0:T(8,128)S(1)}, f32[8,256,1024]{2,1,0:T(8,128)}) fusion(pred[256,1024]{1,0:T(8,128)(4,1)S(1)} %fusion.35, bf16[1024,8,64]{2,0,1:T(8,128)(2,1)} %all-gather.8.cloned.1.call-done, f32[256,8,64]{0,2,1:T(8,128)S(1)} %bitcast.66, f32[64]{0:T(128)S(1)} %copy-done.13, f32[256,8]{0,1:T(8,128)S(1)} %add_rsqrt_fusion), kind=kOutput, calls=%fused_computation.21 | convolution fusion | flops 275118080 | bytes 10240256 | tf_op jit(solution)/shard_map/bhd,jhd->hbj/dot_general | solution.py:123
  559.4 35.3 %all-gather.6.cloned.1.call-done = bf16[1024,8,64]{2,1,0:T(8,128)(2,1)} async-done(((bf16[64,8,64]{2,1,0:T(8,128)(2,1)}), bf16[1024,8,64]{2,1,0:T(8,128)(2,1)}) %all-gather.6.cloned.1.call-update) | async-done | bytes 1048592 | tf_op jit(solution)/shard_map/all_gather | solution.py:116
  594.7 5.5 fusion.41
  601.7 19.2 %reduce-scatter.11.cloned.1.call-done = f32[256,512]{1,0:T(8,128)} async-done(((f32[256,1024]{1,0:T(8,128)}), f32[256,512]{1,0:T(8,128)}) %reduce-scatter.11.cloned.1.call-update) | async-done | bytes 524304 | tf_op jit(solution)/shard_map/reduce_scatter | solution.py:138
  620.9 1.8 add_convert_fusion
  (111 shorter events, 43.0 us)
Async XLA Ops:
  7.2 593.1 %copy-start = (bf16[512,1024]{1,0:T(8,128)(2,1)S(1)}, bf16[512,1024]{1,0:T(8,128)(2,1)}, u32[]{:S(2)}) copy-start(bf16[512,1024]{1,0:T(8,128)(2,1)} %param.33) | copy-start | bytes 3145732
  7.2 56.7 %all-gather.4.cloned.1.call-start = ((), (), s32[]{:S(2)}) async-start(), calls=%async_computation.4 | async-start | bytes 4456448 | tf_op jit(solution)/shard_map/all_gather | solution.py:47
  9.1 283.3 %all-reduce.3.cloned.1.call-start = ((), (), s32[]{:S(2)}) async-start(), calls=%async_computation.5 | async-start | bytes 131072 | tf_op jit(solution)/shard_map/pmax | solution.py:69
  9.1 5.5 copy-start.1
  14.6 3.1 copy-start.5
  14.6 3.2 copy-start.6
  14.6 3.3 copy-start.8
  14.6 3.4 copy-start.10
  207.4 146.2 %reduce-scatter.13.cloned.1.call-start = ((), (), s32[]{:S(2)}) async-start(), calls=%async_computation.11 | async-start | bytes 557056
  294.3 166.0 %reduce-scatter.7.cloned.1.call-start = ((), (), s32[]{:S(2)}) async-start(), calls=%async_computation.6 | async-start | bytes 8912896 | tf_op jit(solution)/shard_map/reduce_scatter | solution.py:72
  302.3 188.3 %reduce-scatter.9.cloned.1.call-start = ((), (), s32[]{:S(2)}) async-start(), calls=%async_computation.7 | async-start | bytes 1572864 | tf_op jit(solution)/shard_map/reduce_scatter | solution.py:84
  470.4 81.8 %all-gather.8.cloned.1.call-start = ((), (), s32[]{:S(2)}) async-start(), calls=%async_computation.9 | async-start | bytes 2228224 | tf_op jit(solution)/shard_map/all_gather | solution.py:115
  470.7 9.4 %copy-start.11 = (f32[4096]{0:T(1024)S(1)}, f32[4096]{0:T(1024)}, u32[]{:S(2)}) copy-start(f32[4096]{0:T(1024)} %param.28) | copy-start | bytes 49156
  470.7 19.9 %copy-start.7 = (bf16[64,2048]{1,0:T(8,128)(2,1)S(1)}, bf16[64,2048]{1,0:T(8,128)(2,1)}, u32[]{:S(2)}) copy-start(bf16[64,2048]{1,0:T(8,128)(2,1)} %param.19) | copy-start | bytes 786436
  491.8 17.6 %copy-start.4 = (bf16[64,2048]{1,0:T(8,128)(2,1)}, bf16[64,2048]{1,0:T(8,128)(2,1)S(1)}, u32[]{:S(2)}) copy-start(bf16[64,2048]{1,0:T(8,128)(2,1)S(1)} %get-tuple-element.95) | copy-start | bytes 786436
  504.3 5.5 copy-start.12
  504.3 7.2 %copy-start.9 = (s32[256]{0:T(256)S(1)}, s32[256]{0:T(256)}, u32[]{:S(2)}) copy-start(s32[256]{0:T(256)} %param.35) | copy-start | bytes 3076
  504.3 7.5 %copy-start.2 = (bf16[256,1024]{1,0:T(8,128)(2,1)S(1)}, bf16[256,1024]{1,0:T(8,128)(2,1)}, u32[]{:S(2)}) copy-start(bf16[256,1024]{1,0:T(8,128)(2,1)} %param.34) | copy-start | bytes 1572868
  504.3 7.5 %copy-start.3 = (bf16[1024,512]{1,0:T(8,128)(2,1)S(1)}, bf16[1024,512]{1,0:T(8,128)(2,1)}, u32[]{:S(2)}) copy-start(bf16[1024,512]{1,0:T(8,128)(2,1)} %param.30) | copy-start | bytes 3145732
  504.3 47.9 %copy-start.13 = (f32[64]{0:T(128)S(1)}, f32[64]{0:T(128)}, u32[]{:S(2)}) copy-start(f32[64]{0:T(128)} %param.31) | copy-start | bytes 772
  510.6 84.0 %all-gather.6.cloned.1.call-start = ((), (), s32[]{:S(2)}) async-start(), calls=%async_computation.8 | async-start | bytes 2228224 | tf_op jit(solution)/shard_map/all_gather | solution.py:116
  511.5 109.4 %reduce-scatter.11.cloned.1.call-start = ((), (), s32[]{:S(2)}) async-start(), calls=%async_computation.10 | async-start | bytes 1572864 | tf_op jit(solution)/shard_map/reduce_scatter | solution.py:138
Sparse Core Ops, SparseCore 0:
  10.7 53.1 all-gather.3
  207.5 84.7 all-reduce.2
  295.9 57.6 reduce-scatter.12
  357.6 102.7 reduce-scatter.6
  470.6 20.0 reduce-scatter.8
  510.8 41.4 all-gather.7
  554.4 40.1 all-gather.5
  601.8 19.0 reduce-scatter.10
where the time goes:
time: 632 us; the launch traced here: 630 us
  waiting for transfers between devices  387 us (61%)
  matrix products  124 us (20%)
  local copies, waits for them, and re-layouts  46.9 us (7%)
  other arithmetic  44.4 us (7%)
  between operations  14.4 us (2%)
  blocking collectives  12.3 us (2%)
    reduce_scatter x1, waiting for transfers between devices, per_device(): lax.psum_scatter(partial_out * factor[..., None], 'ctx', scatter_dimensio...  106 us
    pmax x1, waiting for transfers between devices, per_device(): highest = lax.pmax(partial_max, 'ctx')  84.9 us
    dot_general x16, matrix products, one_head(): jnp.dot(weights.astype(jnp.bfloat16), value_head, preferred_element_type=...  54.4 us
    unnamed x9, waiting for transfers between devices  51.4 us
    all_gather x1, waiting for transfers between devices, per_device(): portion = lax.all_gather(queries, 'ctx', axis=0, tiled=True)  39.9 us
    dot_general x16, matrix products, one_head(): jnp.einsum('qd,kd->qk', query_head, key_head, preferred_element_type=jnp....  39.8 us
    all_gather x1, waiting for transfers between devices, per_device(): piece_keys = lax.all_gather(patch_keys, 'ctx', axis=0, tiled=True)  39.5 us
    all_gather x1, waiting for transfers between devices, per_device(): piece_values = lax.all_gather(patch_values, 'ctx', axis=0, tiled=True)  35.3 us
  transfers between devices with their start and end apart: 8, of which 8 were waited for; matrix products, arithmetic and copies ran while one was open for 7% of the time, Pallas kernels for 0%

commit v1 on v0

--- a/solution.py
+++ b/solution.py
@@ -112,7 +112,12 @@
     owner_table = table_index[None, :] == byte_patch[:, None]
     byte_request = jnp.sum(jnp.where(owner_table, new_request[None, :], 0), axis=1)
     dec_scale = DEC_DH ** (-0.5)
-    piece_keys = lax.all_gather(patch_keys, "ctx", axis=0, tiled=True)
+    ring = [patch_keys]
+    for hop in range(15):
+        ring.append(lax.ppermute(ring[-1], "ctx", [(dev, (dev + 1) % 16) for dev in range(16)]))
+    piece_keys = jnp.roll(
+        jnp.concatenate(ring[::-1], axis=0), (lax.axis_index("ctx") + 1) * ring[0].shape[0], axis=0
+    )
     piece_values = lax.all_gather(patch_values, "ctx", axis=0, tiled=True)
     row_count = piece_keys.shape[0]
     patch_index = jnp.arange(row_count, dtype=jnp.int32)

time: 632 us -> 673 us (1.065)
  waiting for transfers between devices: 387 us -> 414 us
  local copies, waits for them, and re-layouts: 46.9 us -> 60.4 us
    ppermute x0 -> x15, waiting for transfers between devices: none -> 103 us  [per_device(): lax.ppermute(ring[-1], 'ctx', [(dev, (dev + 1) % 16) for dev in range(16)])]
    all_gather x1 -> x0, waiting for transfers between devices: 39.5 us -> none  [per_device(): piece_keys = lax.all_gather(patch_keys, 'ctx', axis=0, tiled=True)]
    all_gather x1, waiting for transfers between devices: 35.3 us -> 0.01 us  [per_device(): piece_values = lax.all_gather(patch_values, 'ctx', axis=0, tiled=True)]
    unnamed x36 -> x66, local copies, waits for them, and re-layouts: 21.7 us -> 28.3 us
    unnamed x9 -> x8, waiting for transfers between devices: 51.4 us -> 51.4 us
  transfers between devices with their start and end apart: 8 -> 22, of which waited for: 8 -> 21; matrix products, arithmetic and copies ran while one was open for 7% -> 7% of each run, Pallas kernels for 0% -> 0%
where the time goes in v1:
time: 673 us; the launch traced here: 671 us
  waiting for transfers between devices  414 us (62%)
  matrix products  124 us (18%)
  local copies, waits for them, and re-layouts  60.4 us (9%)
  other arithmetic  44.5 us (7%)
  between operations  14.5 us (2%)
  blocking collectives  12.3 us (2%)
    reduce_scatter x1, waiting for transfers between devices, per_device(): lax.psum_scatter(partial_out * factor[..., None], 'ctx', scatter_dimensio...  106 us
    ppermute x15, waiting for transfers between devices, per_device(): lax.ppermute(ring[-1], 'ctx', [(dev, (dev + 1) % 16) for dev in range(16)])  103 us
    pmax x1, waiting for transfers between devices, per_device(): highest = lax.pmax(partial_max, 'ctx')  84.9 us
    dot_general x16, matrix products, one_head(): jnp.dot(weights.astype(jnp.bfloat16), value_head, preferred_element_type=...  54.4 us
    unnamed x8, waiting for transfers between devices  51.4 us
    dot_general x16, matrix products, one_head(): jnp.einsum('qd,kd->qk', query_head, key_head, preferred_element_type=jnp....  39.8 us
    all_gather x1, waiting for transfers between devices, per_device(): portion = lax.all_gather(queries, 'ctx', axis=0, tiled=True)  39.8 us
    unnamed x66, local copies, waits for them, and re-layouts  28.3 us
  transfers between devices with their start and end apart: 22, of which 21 were waited for; matrix products, arithmetic and copies ran while one was open for 7% of the time, Pallas kernels for 0%

profile of v1, /device:TPU:0, one launch (start us, length us, event | category | flops | bytes accessed | tf_op | source)
XLA Modules:
  0.0 670.6 jit_solution(14817436686621902664)
XLA Ops:
  9.2 5.4 copy.45
  14.6 3.1 copy.47
  18.0 6.1 maximum_bitcast_fusion
  24.1 39.8 %all-gather.3.cloned.1.call-done = bf16[1024,16,128]{2,0,1:T(8,128)(2,1)} async-done(((bf16[64,16,128]{2,0,1:T(8,128)(2,1)}), bf16[1024,16,128]{2,0,1:T(8,128)(2,1)}) %all-gather.3.cloned.1.call-update) | async-done | bytes 4194320 | tf_op jit(solution)/shard_map/all_gather | solution.py:47
  63.9 143.5 %while.15 = (s32[]{:T(128)}, f32[16,1024,128]{2,1,0:T(8,128)}, f32[16,1024]{1,0:T(8,128)S(1)}, f32[16,1024]{1,0:T(8,128)}, bf16[16,1024,128]{2,1,0:T(8,128)(2,1)...) while((s32[]{:T(128)}, f32[16,1024,128]{2,1,0:T(8,128)}, ...), condition=%wide.region_3.4_spmd.clone, body=%wide.region_0.3_spmd.clone.sunk | while | flops 590477312 | bytes 14786173 | solution.py:67
  63.9 2.5 select_reduce_fusion.3
  66.4 3.4 fusion.67
  72.9 2.5 select_reduce_fusion.3
  75.3 3.4 fusion.67
  81.8 2.5 select_reduce_fusion.3
  84.3 3.4 fusion.67
  90.8 2.5 select_reduce_fusion.3
  93.3 3.4 fusion.67
  99.7 2.5 select_reduce_fusion.3
  102.2 3.4 fusion.67
  108.7 2.5 select_reduce_fusion.3
  111.2 3.4 fusion.67
  117.7 2.5 select_reduce_fusion.3
  120.2 3.4 fusion.67
  126.6 2.5 select_reduce_fusion.3
  129.1 3.4 fusion.67
  135.6 2.5 select_reduce_fusion.3
  138.1 3.4 fusion.67
  144.6 2.5 select_reduce_fusion.3
  147.1 3.4 fusion.67
  153.5 2.5 select_reduce_fusion.3
  156.0 3.4 fusion.67
  162.5 2.5 select_reduce_fusion.3
  165.0 3.4 fusion.67
  174.0 3.4 fusion.67
  180.4 2.5 select_reduce_fusion.3
  182.9 3.4 fusion.67
  191.9 3.4 fusion.67
  198.4 2.5 select_reduce_fusion.3
  200.8 3.4 fusion.67
  207.4 84.9 %all-reduce.3.cloned.1.call-done = f32[16,1024]{1,0:T(8,128)} async-done(((f32[16,1024]{1,0:T(8,128)}), f32[16,1024]{1,0:T(8,128)}) %all-reduce.3.cloned.1.call-update) | async-done | bytes 65552 | tf_op jit(solution)/shard_map/pmax | solution.py:69
  294.3 7.9 %broadcast_multiply_fusion = f32[16,1024,128]{2,1,0:T(8,128)} fusion(f32[16,1024,128]{2,1,0:T(8,128)} %get-tuple-element.46, f32[16,1024]{1,0:T(8,128)S(1)} %get-tuple-element.97), kind=kLoop, calls=%fused_computation.29 | loop fusion | flops 2097152 | bytes 16842752 | tf_op jit(solution)/shard_map/mul | solution.py:72
  302.3 51.3 %reduce-scatter.13.cloned.1.call-done = f32[64,16]{1,0:T(8,128)} async-done(((f32[1024,16]{1,0:T(8,128)}), f32[64,16]{1,0:T(8,128)}) %reduce-scatter.13.cloned.1.call-update) | async-done | bytes 4112
  354.4 105.9 %reduce-scatter.7.cloned.1.call-done = f32[16,64,128]{2,1,0:T(8,128)} async-done(((f32[16,1024,128]{2,1,0:T(8,128)}), f32[16,64,128]{2,1,0:T(8,128)}) %reduce-scatter.7.cloned.1.call-update) | async-done | bytes 524304 | tf_op jit(solution)/shard_map/reduce_scatter | solution.py:72
  460.3 10.1 %convolution_bitcast_fusion = f32[64,4096]{1,0:T(8,128)} fusion(bf16[16,128,4096]{2,1,0:T(8,128)(2,1)} %param.27, f32[16,64,128]{2,1,0:T(8,128)} %reduce-scatter.7.cloned.1.call-done, f32[16,64]{1,0:T(8,128)S(1)} %copy.55), kind=kOutput, calls=%fused_computation.23 | convolution fusion | flops 1074003968 | bytes 18354176 | tf_op jit(solution)/shard_map/dot_general | solution.py:77
  470.7 9.4 %copy.56 = bf16[512,8,2,512]{3,1,2,0:T(8,128)(2,1)} copy(bf16[512,8,2,512]{3,2,1,0:T(2,128)(2,1)} %bitcast.61) | data formatting | bytes 16777216
  480.1 10.5 %reduce-scatter.9.cloned.1.call-done = f32[64,2048]{1,0:T(8,128)} async-done(((f32[64,4096]{1,0:T(8,128)}), f32[64,2048]{1,0:T(8,128)}) %reduce-scatter.9.cloned.1.call-update) | async-done | bytes 524304 | tf_op jit(solution)/shard_map/reduce_scatter | solution.py:84
  491.8 4.9 psum.7
  496.9 7.4 %all_gather.10 = bf16[64,4096]{1,0:T(8,128)(2,1)S(1)} all-gather(bf16[64,2048]{1,0:T(8,128)(2,1)S(1)} %fusion.40), channel_id=1, replica_groups=mesh['ctx'=16,'head'=2] {'head'}, dimensions={1}, use_global_device_ids=true | all-gather | bytes 786432 | tf_op jit(solution)/shard_map/all_gather | solution.py:92
  504.3 5.1 fusion.52
  510.8 7.1 %collective-permute-done = bf16[64,8,64]{0,2,1:T(8,128)(2,1)S(1)} collective-permute-done((bf16[64,8,64]{0,2,1:T(8,128)(2,1)S(1)}, bf16[64,8,64]{0,2,1:T(8,128)(2,1)S(1)}, u32[]{:S(2)}, u32[]{:S(2)}) %collective-permute-start) | collective-permute-done | bytes 65568 | tf_op jit(solution)/shard_map/ppermute | solution.py:117
  519.6 5.3 collective-permute-done.1
  524.9 7.2 %collective-permute-done.2 = bf16[64,8,64]{0,2,1:T(8,128)(2,1)S(1)} collective-permute-done((bf16[64,8,64]{0,2,1:T(8,128)(2,1)S(1)}, bf16[64,8,64]{0,2,1:T(8,128)(2,1)S(1)}, u32[]{:S(2)}, u32[]{:S(2)}) %collective-permute-start.2) | collective-permute-done | bytes 65568 | tf_op jit(solution)/shard_map/ppermute | solution.py:117
  532.1 7.8 %collective-permute-done.3 = bf16[64,8,64]{0,2,1:T(8,128)(2,1)S(1)} collective-permute-done((bf16[64,8,64]{0,2,1:T(8,128)(2,1)S(1)}, bf16[64,8,64]{0,2,1:T(8,128)(2,1)S(1)}, u32[]{:S(2)}, u32[]{:S(2)}) %collective-permute-start.3) | collective-permute-done | bytes 65568 | tf_op jit(solution)/shard_map/ppermute | solution.py:117
  539.9 7.1 %collective-permute-done.4 = bf16[64,8,64]{0,2,1:T(8,128)(2,1)S(1)} collective-permute-done((bf16[64,8,64]{0,2,1:T(8,128)(2,1)S(1)}, bf16[64,8,64]{0,2,1:T(8,128)(2,1)S(1)}, u32[]{:S(2)}, u32[]{:S(2)}) %collective-permute-start.4) | collective-permute-done | bytes 65568 | tf_op jit(solution)/shard_map/ppermute | solution.py:117
  547.7 8.3 %collective-permute-done.5 = bf16[64,8,64]{0,2,1:T(8,128)(2,1)S(1)} collective-permute-done((bf16[64,8,64]{0,2,1:T(8,128)(2,1)S(1)}, bf16[64,8,64]{0,2,1:T(8,128)(2,1)S(1)}, u32[]{:S(2)}, u32[]{:S(2)}) %collective-permute-start.5) | collective-permute-done | bytes 65568 | tf_op jit(solution)/shard_map/ppermute | solution.py:117
  556.6 7.1 %collective-permute-done.6 = bf16[64,8,64]{0,2,1:T(8,128)(2,1)S(1)} collective-permute-done((bf16[64,8,64]{0,2,1:T(8,128)(2,1)S(1)}, bf16[64,8,64]{0,2,1:T(8,128)(2,1)S(1)}, u32[]{:S(2)}, u32[]{:S(2)}) %collective-permute-start.6) | collective-permute-done | bytes 65568 | tf_op jit(solution)/shard_map/ppermute | solution.py:117
  564.4 7.1 %collective-permute-done.7 = bf16[64,8,64]{0,2,1:T(8,128)(2,1)S(1)} collective-permute-done((bf16[64,8,64]{0,2,1:T(8,128)(2,1)S(1)}, bf16[64,8,64]{0,2,1:T(8,128)(2,1)S(1)}, u32[]{:S(2)}, u32[]{:S(2)}) %collective-permute-start.7) | collective-permute-done | bytes 65568 | tf_op jit(solution)/shard_map/ppermute | solution.py:117
  572.1 7.1 %collective-permute-done.8 = bf16[64,8,64]{0,2,1:T(8,128)(2,1)S(1)} collective-permute-done((bf16[64,8,64]{0,2,1:T(8,128)(2,1)S(1)}, bf16[64,8,64]{0,2,1:T(8,128)(2,1)S(1)}, u32[]{:S(2)}, u32[]{:S(2)}) %collective-permute-start.8) | collective-permute-done | bytes 65568 | tf_op jit(solution)/shard_map/ppermute | solution.py:117
  579.9 7.1 %collective-permute-done.9 = bf16[64,8,64]{0,2,1:T(8,128)(2,1)S(1)} collective-permute-done((bf16[64,8,64]{0,2,1:T(8,128)(2,1)S(1)}, bf16[64,8,64]{0,2,1:T(8,128)(2,1)S(1)}, u32[]{:S(2)}, u32[]{:S(2)}) %collective-permute-start.9) | collective-permute-done | bytes 65568 | tf_op jit(solution)/shard_map/ppermute | solution.py:117
  587.6 7.1 %collective-permute-done.10 = bf16[64,8,64]{0,2,1:T(8,128)(2,1)S(1)} collective-permute-done((bf16[64,8,64]{0,2,1:T(8,128)(2,1)S(1)}, bf16[64,8,64]{0,2,1:T(8,128)(2,1)S(1)}, u32[]{:S(2)}, u32[]{:S(2)}) %collective-permute-start.10) | collective-permute-done | bytes 65568 | tf_op jit(solution)/shard_map/ppermute | solution.py:117
  596.0 5.7 collective-permute-done.11
  602.7 6.8 %collective-permute-done.12 = bf16[64,8,64]{0,2,1:T(8,128)(2,1)S(1)} collective-permute-done((bf16[64,8,64]{0,2,1:T(8,128)(2,1)S(1)}, bf16[64,8,64]{0,2,1:T(8,128)(2,1)S(1)}, u32[]{:S(2)}, u32[]{:S(2)}) %collective-permute-start.12) | collective-permute-done | bytes 65568 | tf_op jit(solution)/shard_map/ppermute | solution.py:117
  611.3 6.0 collective-permute-done.13
  617.9 6.6 collective-permute-done.14
  624.5 5.9 concatenate.22
  630.4 6.7 fusion.22
  637.1 5.6 divide_convert_fusion
  644.2 17.8 %reduce-scatter.11.cloned.1.call-done = f32[256,512]{1,0:T(8,128)} async-done(((f32[256,1024]{1,0:T(8,128)}), f32[256,512]{1,0:T(8,128)}) %reduce-scatter.11.cloned.1.call-update) | async-done | bytes 524304 | tf_op jit(solution)/shard_map/reduce_scatter | solution.py:143
  (170 shorter events, 75.4 us)
Async XLA Ops:
  7.2 635.5 %copy-start = (bf16[512,1024]{1,0:T(8,128)(2,1)S(1)}, bf16[512,1024]{1,0:T(8,128)(2,1)}, u32[]{:S(2)}) copy-start(bf16[512,1024]{1,0:T(8,128)(2,1)} %param.33) | copy-start | bytes 3145732
  7.2 56.7 %all-gather.3.cloned.1.call-start = ((), (), s32[]{:S(2)}) async-start(), calls=%async_computation.4 | async-start | bytes 4456448 | tf_op jit(solution)/shard_map/all_gather | solution.py:47
  9.1 283.3 %all-reduce.3.cloned.1.call-start = ((), (), s32[]{:S(2)}) async-start(), calls=%async_computation.5 | async-start | bytes 131072 | tf_op jit(solution)/shard_map/pmax | solution.py:69
  9.1 5.4 copy-start.1
  14.6 3.2 copy-start.19
  14.6 3.2 copy-start.20
  14.6 3.3 copy-start.23
  14.6 3.4 copy-start.25
  207.4 146.2 %reduce-scatter.13.cloned.1.call-start = ((), (), s32[]{:S(2)}) async-start(), calls=%async_computation.10 | async-start | bytes 557056
  294.3 166.1 %reduce-scatter.7.cloned.1.call-start = ((), (), s32[]{:S(2)}) async-start(), calls=%async_computation.6 | async-start | bytes 8912896 | tf_op jit(solution)/shard_map/reduce_scatter | solution.py:72
  302.3 188.3 %reduce-scatter.9.cloned.1.call-start = ((), (), s32[]{:S(2)}) async-start(), calls=%async_computation.7 | async-start | bytes 1572864 | tf_op jit(solution)/shard_map/reduce_scatter | solution.py:84
  470.4 166.7 %all-gather.5.cloned.1.call-start = ((), (), s32[]{:S(2)}) async-start(), calls=%async_computation.8 | async-start | bytes 2228224 | tf_op jit(solution)/shard_map/all_gather | solution.py:121
  470.7 9.4 %copy-start.26 = (f32[4096]{0:T(1024)S(1)}, f32[4096]{0:T(1024)}, u32[]{:S(2)}) copy-start(f32[4096]{0:T(1024)} %param.28) | copy-start | bytes 49156
  470.7 19.9 %copy-start.22 = (bf16[64,2048]{1,0:T(8,128)(2,1)S(1)}, bf16[64,2048]{1,0:T(8,128)(2,1)}, u32[]{:S(2)}) copy-start(bf16[64,2048]{1,0:T(8,128)(2,1)} %param.19) | copy-start | bytes 786436
  491.8 17.6 %copy-start.5 = (bf16[64,2048]{1,0:T(8,128)(2,1)}, bf16[64,2048]{1,0:T(8,128)(2,1)S(1)}, u32[]{:S(2)}) copy-start(bf16[64,2048]{1,0:T(8,128)(2,1)S(1)} %get-tuple-element.95) | copy-start | bytes 786436
  504.3 6.3 copy-start.27
  504.3 90.4 %copy-start.2 = (bf16[256,1024]{1,0:T(8,128)(2,1)S(1)}, bf16[256,1024]{1,0:T(8,128)(2,1)}, u32[]{:S(2)}) copy-start(bf16[256,1024]{1,0:T(8,128)(2,1)} %param.34) | copy-start | bytes 1572868
  504.3 90.4 %copy-start.4 = (bf16[1024,512]{1,0:T(8,128)(2,1)S(1)}, bf16[1024,512]{1,0:T(8,128)(2,1)}, u32[]{:S(2)}) copy-start(bf16[1024,512]{1,0:T(8,128)(2,1)} %param.30) | copy-start | bytes 3145732
  509.4 0.7 copy-start.6
  509.4 93.0 %copy-start.24 = (s32[256]{0:T(256)S(1)}, s32[256]{0:T(256)}, u32[]{:S(2)}) copy-start(s32[256]{0:T(256)} %param.35) | copy-start | bytes 3076
  510.7 7.1 %collective-permute-start = (bf16[64,8,64]{0,2,1:T(8,128)(2,1)S(1)}, bf16[64,8,64]{0,2,1:T(8,128)(2,1)S(1)}, u32[]{:S(2)}, u32[]{:S(2)}) collective-permute-start(bf16[64,8,64]{0,2,1:T(8,128)(2,1)S(1)} %multiply_convert_fusion.2), channel_id=1, source_target_pairs={{0,2},{2,4},{4,6},{6,8},{8,10},{10,12},{12,14},{14,16},{16,18},{18... | collective-permute-start | bytes 196616 | tf_op jit(solution)/shard_map/ppermute | solution.py:117
  517.8 7.1 %collective-permute-start.1 = (bf16[64,8,64]{0,2,1:T(8,128)(2,1)S(1)}, bf16[64,8,64]{0,2,1:T(8,128)(2,1)S(1)}, u32[]{:S(2)}, u32[]{:S(2)}) collective-permute-start(bf16[64,8,64]{0,2,1:T(8,128)(2,1)S(1)} %collective-permute-done), channel_id=1, source_target_pairs={{0,2},{2,4},{4,6},{6,8},{8,10},{10,12},{12,14},{14,16},{16,18},{18... | collective-permute-start | bytes 196616 | tf_op jit(solution)/shard_map/ppermute | solution.py:117
  519.5 110.8 %copy-start.28 = (f32[64]{0:T(128)S(1)}, f32[64]{0:T(128)}, u32[]{:S(2)}) copy-start(f32[64]{0:T(128)} %param.31) | copy-start | bytes 772
  519.6 142.4 %reduce-scatter.11.cloned.1.call-start = ((), (), s32[]{:S(2)}) async-start(), calls=%async_computation.9 | async-start | bytes 1572864 | tf_op jit(solution)/shard_map/reduce_scatter | solution.py:143
  524.9 7.2 %collective-permute-start.2 = (bf16[64,8,64]{0,2,1:T(8,128)(2,1)S(1)}, bf16[64,8,64]{0,2,1:T(8,128)(2,1)S(1)}, u32[]{:S(2)}, u32[]{:S(2)}) collective-permute-start(bf16[64,8,64]{0,2,1:T(8,128)(2,1)S(1)} %collective-permute-done.1), channel_id=1, source_target_pairs={{0,2},{2,4},{4,6},{6,8},{8,10},{10,12},{12,14},{14,16},{16,18},{18... | collective-permute-start | bytes 196616 | tf_op jit(solution)/shard_map/ppermute | solution.py:117
  532.1 85.2 %copy-start.7 = (bf16[64,8,64]{0,2,1:T(8,128)(2,1)}, bf16[64,8,64]{0,2,1:T(8,128)(2,1)S(1)}, u32[]{:S(2)}) copy-start(bf16[64,8,64]{0,2,1:T(8,128)(2,1)S(1)} %collective-permute-done.2) | copy-start | bytes 196612
  532.1 7.8 %collective-permute-start.3 = (bf16[64,8,64]{0,2,1:T(8,128)(2,1)S(1)}, bf16[64,8,64]{0,2,1:T(8,128)(2,1)S(1)}, u32[]{:S(2)}, u32[]{:S(2)}) collective-permute-start(bf16[64,8,64]{0,2,1:T(8,128)(2,1)S(1)} %collective-permute-done.2), channel_id=1, source_target_pairs={{0,2},{2,4},{4,6},{6,8},{8,10},{10,12},{12,14},{14,16},{16,18},{18... | collective-permute-start | bytes 196616 | tf_op jit(solution)/shard_map/ppermute | solution.py:117
  539.9 77.4 %copy-start.8 = (bf16[64,8,64]{0,2,1:T(8,128)(2,1)}, bf16[64,8,64]{0,2,1:T(8,128)(2,1)S(1)}, u32[]{:S(2)}) copy-start(bf16[64,8,64]{0,2,1:T(8,128)(2,1)S(1)} %collective-permute-done.3) | copy-start | bytes 196612
  539.9 7.1 %collective-permute-start.4 = (bf16[64,8,64]{0,2,1:T(8,128)(2,1)S(1)}, bf16[64,8,64]{0,2,1:T(8,128)(2,1)S(1)}, u32[]{:S(2)}, u32[]{:S(2)}) collective-permute-start(bf16[64,8,64]{0,2,1:T(8,128)(2,1)S(1)} %collective-permute-done.3), channel_id=1, source_target_pairs={{0,2},{2,4},{4,6},{6,8},{8,10},{10,12},{12,14},{14,16},{16,18},{18... | collective-permute-start | bytes 196616 | tf_op jit(solution)/shard_map/ppermute | solution.py:117
  547.0 0.7 copy-start.9
  547.7 8.3 %collective-permute-start.5 = (bf16[64,8,64]{0,2,1:T(8,128)(2,1)S(1)}, bf16[64,8,64]{0,2,1:T(8,128)(2,1)S(1)}, u32[]{:S(2)}, u32[]{:S(2)}) collective-permute-start(bf16[64,8,64]{0,2,1:T(8,128)(2,1)S(1)} %collective-permute-done.4), channel_id=1, source_target_pairs={{0,2},{2,4},{4,6},{6,8},{8,10},{10,12},{12,14},{14,16},{16,18},{18... | collective-permute-start | bytes 196616 | tf_op jit(solution)/shard_map/ppermute | solution.py:117
  556.0 0.7 copy-start.10
  556.6 7.1 %collective-permute-start.6 = (bf16[64,8,64]{0,2,1:T(8,128)(2,1)S(1)}, bf16[64,8,64]{0,2,1:T(8,128)(2,1)S(1)}, u32[]{:S(2)}, u32[]{:S(2)}) collective-permute-start(bf16[64,8,64]{0,2,1:T(8,128)(2,1)S(1)} %collective-permute-done.5), channel_id=1, source_target_pairs={{0,2},{2,4},{4,6},{6,8},{8,10},{10,12},{12,14},{14,16},{16,18},{18... | collective-permute-start | bytes 196616 | tf_op jit(solution)/shard_map/ppermute | solution.py:117
  563.7 0.6 copy-start.11
  564.4 7.1 %collective-permute-start.7 = (bf16[64,8,64]{0,2,1:T(8,128)(2,1)S(1)}, bf16[64,8,64]{0,2,1:T(8,128)(2,1)S(1)}, u32[]{:S(2)}, u32[]{:S(2)}) collective-permute-start(bf16[64,8,64]{0,2,1:T(8,128)(2,1)S(1)} %collective-permute-done.6), channel_id=1, source_target_pairs={{0,2},{2,4},{4,6},{6,8},{8,10},{10,12},{12,14},{14,16},{16,18},{18... | collective-permute-start | bytes 196616 | tf_op jit(solution)/shard_map/ppermute | solution.py:117
  571.5 0.7 copy-start.12
  572.1 7.1 %collective-permute-start.8 = (bf16[64,8,64]{0,2,1:T(8,128)(2,1)S(1)}, bf16[64,8,64]{0,2,1:T(8,128)(2,1)S(1)}, u32[]{:S(2)}, u32[]{:S(2)}) collective-permute-start(bf16[64,8,64]{0,2,1:T(8,128)(2,1)S(1)} %collective-permute-done.7), channel_id=1, source_target_pairs={{0,2},{2,4},{4,6},{6,8},{8,10},{10,12},{12,14},{14,16},{16,18},{18... | collective-permute-start | bytes 196616 | tf_op jit(solution)/shard_map/ppermute | solution.py:117
  579.2 0.7 copy-start.13
  579.9 7.1 %collective-permute-start.9 = (bf16[64,8,64]{0,2,1:T(8,128)(2,1)S(1)}, bf16[64,8,64]{0,2,1:T(8,128)(2,1)S(1)}, u32[]{:S(2)}, u32[]{:S(2)}) collective-permute-start(bf16[64,8,64]{0,2,1:T(8,128)(2,1)S(1)} %collective-permute-done.8), channel_id=1, source_target_pairs={{0,2},{2,4},{4,6},{6,8},{8,10},{10,12},{12,14},{14,16},{16,18},{18... | collective-permute-start | bytes 196616 | tf_op jit(solution)/shard_map/ppermute | solution.py:117
  587.0 0.6 copy-start.14
  587.6 7.1 %collective-permute-start.10 = (bf16[64,8,64]{0,2,1:T(8,128)(2,1)S(1)}, bf16[64,8,64]{0,2,1:T(8,128)(2,1)S(1)}, u32[]{:S(2)}, u32[]{:S(2)}) collective-permute-start(bf16[64,8,64]{0,2,1:T(8,128)(2,1)S(1)} %collective-permute-done.9), channel_id=1, source_target_pairs={{0,2},{2,4},{4,6},{6,8},{8,10},{10,12},{12,14},{14,16},{16,18},{18... | collective-permute-start | bytes 196616 | tf_op jit(solution)/shard_map/ppermute | solution.py:117
  594.7 1.4 copy-start.15
  594.7 7.1 %collective-permute-start.11 = (bf16[64,8,64]{0,2,1:T(8,128)(2,1)S(1)}, bf16[64,8,64]{0,2,1:T(8,128)(2,1)S(1)}, u32[]{:S(2)}, u32[]{:S(2)}) collective-permute-start(bf16[64,8,64]{0,2,1:T(8,128)(2,1)S(1)} %collective-permute-done.10), channel_id=1, source_target_pairs={{0,2},{2,4},{4,6},{6,8},{8,10},{10,12},{12,14},{14,16},{16,18},{18... | collective-permute-start | bytes 196616 | tf_op jit(solution)/shard_map/ppermute | solution.py:117
  601.8 0.7 copy-start.16
  602.4 7.1 %collective-permute-start.12 = (bf16[64,8,64]{0,2,1:T(8,128)(2,1)S(1)}, bf16[64,8,64]{0,2,1:T(8,128)(2,1)S(1)}, u32[]{:S(2)}, u32[]{:S(2)}) collective-permute-start(bf16[64,8,64]{0,2,1:T(8,128)(2,1)S(1)} %collective-permute-done.11), channel_id=1, source_target_pairs={{0,2},{2,4},{4,6},{6,8},{8,10},{10,12},{12,14},{14,16},{16,18},{18... | collective-permute-start | bytes 196616 | tf_op jit(solution)/shard_map/ppermute | solution.py:117
  609.5 0.6 copy-start.17
  610.2 7.1 %collective-permute-start.13 = (bf16[64,8,64]{0,2,1:T(8,128)(2,1)S(1)}, bf16[64,8,64]{0,2,1:T(8,128)(2,1)S(1)}, u32[]{:S(2)}, u32[]{:S(2)}) collective-permute-start(bf16[64,8,64]{0,2,1:T(8,128)(2,1)S(1)} %collective-permute-done.12), channel_id=1, source_target_pairs={{0,2},{2,4},{4,6},{6,8},{8,10},{10,12},{12,14},{14,16},{16,18},{18... | collective-permute-start | bytes 196616 | tf_op jit(solution)/shard_map/ppermute | solution.py:117
  617.3 0.6 copy-start.18
  617.3 7.2 %collective-permute-start.14 = (bf16[64,8,64]{0,2,1:T(8,128)(2,1)S(1)}, bf16[64,8,64]{0,2,1:T(8,128)(2,1)}, u32[]{:S(2)}, u32[]{:S(2)}) collective-permute-start(bf16[64,8,64]{0,2,1:T(8,128)(2,1)S(1)} %collective-permute-done.13), channel_id=1, source_target_pairs={{0,2},{2,4},{4,6},{6,8},{8,10},{10,12},{12,14},{14,16},{16,18},{18... | collective-permute-start | bytes 196616 | tf_op jit(solution)/shard_map/ppermute | solution.py:117
  630.4 6.7 %copy-start.21 = (pred[256,1024]{1,0:T(8,128)(4,1)S(1)}, pred[256,1024]{1,0:T(8,128)(4,1)}, u32[]{:S(2)}) copy-start(pred[256,1024]{1,0:T(8,128)(4,1)} %fusion.37) | copy-start | bytes 786436
  637.1 24.9 %copy-start.3 = (bf16[256,1024]{1,0:T(8,128)(2,1)S(1)}, bf16[256,1024]{1,0:T(8,128)(2,1)}, u32[]{:S(2)}) copy-start(bf16[256,1024]{1,0:T(8,128)(2,1)} %param.34) | copy-start | bytes 1572868
Sparse Core Ops, SparseCore 0:
  10.7 53.1 all-gather.2
  207.5 84.7 all-reduce.2
  295.9 57.6 reduce-scatter.12
  357.6 102.7 reduce-scatter.6
  470.5 20.0 reduce-scatter.8
  519.7 43.4 all-gather.4
  644.3 17.5 reduce-scatter.10
